TPU v7x, 32 devices: a whole 2x2x4 slice. The times are simulated.
32 devices in a mesh: node: 4 (over y, x), row: 8 (over z, core).
Axes of the slice: x: 2, y: 2, z: 4, core: 2. Of those that a mesh axis runs over, the one named last changes fastest.
Arguments:
- inputs: float32 [16, 32, 128, 128], P(None, 'row'), may hold values from -8 to 8
- diagonal: float32 [32, 128, 128], P('row'), may hold values from 0.05 to 1
- observations: float32 [16, 32, 128, 128], P(None, 'row'), may hold values from -0.0078125 to 0.0078125
- frequencies: float32 [4], replicated, may hold values from 0.2 to 3
- weights: float32 [4], replicated, may hold values from 0.5 to 2
- counts: int32 [4], replicated, may hold values from 3 to 6, as said below
- assignment: int32 [4], replicated, may hold values from 0 to 3, each once
Outputs:
- probe_response: float32 [16, 32, 128, 128], P(None, 'row')
- group_gram: float32 [4, 16, 16], P('node')
Inputs may be any that keep to these rules, and one draw needn't show every extreme that they name: `counts`: some node has 6 sweeps and some node 3 in every draw. `assignment`: each node 0 to 3 appears once.
All inputs are finite; a program needn't handle non-finite values.
Results may differ from a plain program's by a relative error of at most 0.0003.
Values sent between devices are 32-bit elements; how exact they have to be, the bound alone decides.
A program may use at most 192 MiB of HBM per device.

v0:
```python
import jax
import jax.numpy as jnp
from jax import lax
from jax.sharding import PartitionSpec as P

NODE_DEV = 1
ITERS = 6


def with_halo(block, sides, width):
    for axis, dim in sides:
        count = lax.axis_size(axis)
        forward = [(i, i + 1) for i in range(count - 1)]
        backward = [(target, source) for source, target in forward]
        low = lax.ppermute(
            lax.slice_in_dim(block, block.shape[dim] - width, None, axis=dim), axis, forward
        )
        high = lax.ppermute(lax.slice_in_dim(block, 0, width, axis=dim), axis, backward)
        block = jnp.concatenate([low, block, high], axis=dim)
    return block


def relax_step(fields, beyond, source, diagonal, shift_col, active):
    padded = jnp.pad(fields, ((0, 0), (0, 0), (0, 0), (0, 0), (1, 1), (1, 1)))
    beside = beyond[:, :, :, 2:] + beyond[:, :, :, :-2]
    beside = beside + padded[:, :, :, :, 2:, 1:-1] + padded[:, :, :, :, :-2, 1:-1]
    beside = beside + padded[:, :, :, :, 1:-1, 2:] + padded[:, :, :, :, 1:-1, :-2]
    diag_full = 6.0 + diagonal
    applied = diag_full * fields - beside
    resid_real = source - applied[:, 0] + shift_col * fields[:, 1]
    resid_imag = -applied[:, 1] - shift_col * fields[:, 0]
    denominator = diag_full * diag_full + shift_col * shift_col
    step_real = (diag_full * resid_real + shift_col * resid_imag) / denominator
    step_imag = (diag_full * resid_imag - shift_col * resid_real) / denominator
    return fields + active * jnp.stack([step_real, step_imag], 1)


def local(inputs, diagonal, observations, frequencies, weights, counts, assignment):
    group_id = lax.axis_index("node")
    my_nodes = lax.dynamic_slice_in_dim(assignment, group_id * NODE_DEV, NODE_DEV)
    quad_count = frequencies.shape[0]
    lookup = my_nodes[:, None] == jnp.arange(quad_count, dtype=jnp.int32)[None, :]
    my_freqs = jnp.sum(jnp.where(lookup, frequencies[None, :], 0.0), 1)
    my_weights = jnp.sum(jnp.where(lookup, weights[None, :], 0.0), 1)
    my_counts = jnp.sum(jnp.where(lookup, counts[None, :], 0), 1)
    planes = inputs.shape[1]
    shift_col = my_freqs.reshape(NODE_DEV, 1, 1, 1, 1)
    start_fields = jnp.zeros((NODE_DEV, 2) + inputs.shape, jnp.float32)

    def sweep_once(sweep, fields):
        beyond = with_halo(fields, (("row", 3),), 1)
        active = (sweep < my_counts).astype(jnp.float32).reshape(NODE_DEV, 1, 1, 1, 1, 1)
        return relax_step(fields, beyond, inputs, diagonal, shift_col, active)

    fields = lax.fori_loop(0, ITERS, sweep_once, start_fields)
    local_cells = planes * inputs.shape[2] * inputs.shape[3]
    flat_fields = fields.reshape(NODE_DEV, 2, inputs.shape[0], local_cells)
    flat_probe = observations.reshape(observations.shape[0], local_cells)
    projected = jnp.einsum(
        "naic,pc->naip", flat_fields, flat_probe, precision=lax.Precision.HIGHEST
    )
    gram_part = jnp.einsum(
        "naic,najc->nij", flat_fields, flat_fields, precision=lax.Precision.HIGHEST
    )
    projected, gram_part = lax.psum((projected, gram_part), "row")
    total_cells = local_cells * lax.axis_size("row")
    group_gram = (
        jnp.einsum("n,nij->ij", my_weights, gram_part, precision=lax.Precision.HIGHEST)
        / total_cells
    )
    weighted = projected * my_weights.reshape(NODE_DEV, 1, 1, 1)
    share = jnp.einsum("naip,naic->pc", weighted, flat_fields, precision=lax.Precision.HIGHEST)
    summed = lax.psum(share, "node")
    probe_response = (summed / quad_count).reshape(observations.shape)
    return (probe_response, group_gram[None])


def solution(mesh):
    placed = (
        P(None, "row", None, None),
        P("row", None, None),
        P(None, "row", None, None),
        P(),
        P(),
        P(),
        P(),
    )
    return jax.shard_map(
        local,
        mesh=mesh,
        in_specs=placed,
        out_specs=(P(None, "row", None, None), P("node", None, None)),
        check_vma=False,
    )
```

profile of v0, /device:TPU:0, one launch (start us, length us, event | category | flops | bytes accessed | tf_op | source)
XLA Modules:
  0.0 677.6 jit_solution(16696439240070895874)
XLA Ops:
  13.5 447.5 %while.16 = (s32[]{:T(128)}, f32[1,2,16,4,128,128]{5,4,3,2,1,0:T(8,128)}, s32[1]{0:T(128)}, f32[4,128,128]{2,1,0:T(8,128)}, f32[16,4,128,128]{3,2,1,0:T(8,128)},...) while((s32[]{:T(128)}, ...), condition=%wide.region_3.4_spmd.clone, body=%wide.region_2.3_spmd.clone.sunk | while | flops 44236800 | bytes 237502864 | solution.py:55
  30.0 24.3 %fusion.25 = f32[1,2,16,4,128,128]{5,4,3,2,1,0:T(8,128)S(1)} fusion(f32[1,2,16,4,128,128]{5,4,3,2,1,0:T(8,128)} %copy-done, f32[1,2,16,1,128,128]{5,4,3,2,1,0:T(8,128)} %collective-permute-done, f32[1,2,16,1,128,128]{5,4,3,2,1,0:T(8,128)} %collective-permute-done.1, f32[4,128,128]{2,1,0:T(8,128)} %get-tuple-element.259), kind=kLoop, calls=%fused_computation.8.clone.1 | loop fusion | flops 18874368 | bytes 21233664 | tf_op jit(solution)/shard_map/while/body/eval_jaxpr/sub | solution.py:29
  54.3 7.1 %add_divide_fusion.2 = (f32[1,1,16,4,128,128]{5,4,3,2,1,0:T(8,128)}, f32[1,1,16,4,128,128]{5,4,3,2,1,0:T(8,128)}) fusion(f32[4,128,128]{2,1,0:T(8,128)} %get-tuple-element.258, f32[]{:T(128)} %bitcast.45, f32[4,128,128]{2,1,0:T(8,128)} %get-tuple-element.259, f32[1,2,16,4,128,128]{5,4,3,2,1,0:T(8,128)S(1)} %bitcast.49, ...), kind=kLoop, calls=%fused_computation.22.clone.1 | loop fusion | flops 14680064 | bytes 29884420 | tf_op jit(solution)/shard_map/while/body/eval_jaxpr/div | solution.py:33
  78.6 25.0 %collective-permute-start = (f32[1,2,16,1,128,128]{5,4,3,2,1,0:T(8,128)}, f32[1,2,16,1,128,128]{5,4,3,2,1,0:T(8,128)}, u32[]{:S(2)}, u32[]{:S(2)}) collective-permute-start(f32[1,2,16,1,128,128]{5,4,3,2,1,0:T(8,128)} %get-tuple-element.260), channel_id=1, source_target_pairs={{0,1},{1,2},{2,3},{3,4},{4,5},{5,6},{6,7},{8,9},{9,10},{10,11},{11... | collective-permute-start | bytes 6291464 | tf_op jit(solution)/shard_map/while/body/eval_jaxpr/ppermute | solution.py:15
  109.8 24.3 %fusion.25 = f32[1,2,16,4,128,128]{5,4,3,2,1,0:T(8,128)S(1)} fusion(f32[1,2,16,4,128,128]{5,4,3,2,1,0:T(8,128)} %copy-done, f32[1,2,16,1,128,128]{5,4,3,2,1,0:T(8,128)} %collective-permute-done, f32[1,2,16,1,128,128]{5,4,3,2,1,0:T(8,128)} %collective-permute-done.1, f32[4,128,128]{2,1,0:T(8,128)} %get-tuple-element.259), kind=kLoop, calls=%fused_computation.8.clone.1 | loop fusion | flops 18874368 | bytes 21233664 | tf_op jit(solution)/shard_map/while/body/eval_jaxpr/sub | solution.py:29
  134.1 7.1 %add_divide_fusion.2 = (f32[1,1,16,4,128,128]{5,4,3,2,1,0:T(8,128)}, f32[1,1,16,4,128,128]{5,4,3,2,1,0:T(8,128)}) fusion(f32[4,128,128]{2,1,0:T(8,128)} %get-tuple-element.258, f32[]{:T(128)} %bitcast.45, f32[4,128,128]{2,1,0:T(8,128)} %get-tuple-element.259, f32[1,2,16,4,128,128]{5,4,3,2,1,0:T(8,128)S(1)} %bitcast.49, ...), kind=kLoop, calls=%fused_computation.22.clone.1 | loop fusion | flops 14680064 | bytes 29884420 | tf_op jit(solution)/shard_map/while/body/eval_jaxpr/div | solution.py:33
  158.3 23.2 %collective-permute-start = (f32[1,2,16,1,128,128]{5,4,3,2,1,0:T(8,128)}, f32[1,2,16,1,128,128]{5,4,3,2,1,0:T(8,128)}, u32[]{:S(2)}, u32[]{:S(2)}) collective-permute-start(f32[1,2,16,1,128,128]{5,4,3,2,1,0:T(8,128)} %get-tuple-element.260), channel_id=1, source_target_pairs={{0,1},{1,2},{2,3},{3,4},{4,5},{5,6},{6,7},{8,9},{9,10},{10,11},{11... | collective-permute-start | bytes 6291464 | tf_op jit(solution)/shard_map/while/body/eval_jaxpr/ppermute | solution.py:15
  187.7 24.3 %fusion.25 = f32[1,2,16,4,128,128]{5,4,3,2,1,0:T(8,128)S(1)} fusion(f32[1,2,16,4,128,128]{5,4,3,2,1,0:T(8,128)} %copy-done, f32[1,2,16,1,128,128]{5,4,3,2,1,0:T(8,128)} %collective-permute-done, f32[1,2,16,1,128,128]{5,4,3,2,1,0:T(8,128)} %collective-permute-done.1, f32[4,128,128]{2,1,0:T(8,128)} %get-tuple-element.259), kind=kLoop, calls=%fused_computation.8.clone.1 | loop fusion | flops 18874368 | bytes 21233664 | tf_op jit(solution)/shard_map/while/body/eval_jaxpr/sub | solution.py:29
  212.0 7.1 %add_divide_fusion.2 = (f32[1,1,16,4,128,128]{5,4,3,2,1,0:T(8,128)}, f32[1,1,16,4,128,128]{5,4,3,2,1,0:T(8,128)}) fusion(f32[4,128,128]{2,1,0:T(8,128)} %get-tuple-element.258, f32[]{:T(128)} %bitcast.45, f32[4,128,128]{2,1,0:T(8,128)} %get-tuple-element.259, f32[1,2,16,4,128,128]{5,4,3,2,1,0:T(8,128)S(1)} %bitcast.49, ...), kind=kLoop, calls=%fused_computation.22.clone.1 | loop fusion | flops 14680064 | bytes 29884420 | tf_op jit(solution)/shard_map/while/body/eval_jaxpr/div | solution.py:33
  236.3 23.2 %collective-permute-start = (f32[1,2,16,1,128,128]{5,4,3,2,1,0:T(8,128)}, f32[1,2,16,1,128,128]{5,4,3,2,1,0:T(8,128)}, u32[]{:S(2)}, u32[]{:S(2)}) collective-permute-start(f32[1,2,16,1,128,128]{5,4,3,2,1,0:T(8,128)} %get-tuple-element.260), channel_id=1, source_target_pairs={{0,1},{1,2},{2,3},{3,4},{4,5},{5,6},{6,7},{8,9},{9,10},{10,11},{11... | collective-permute-start | bytes 6291464 | tf_op jit(solution)/shard_map/while/body/eval_jaxpr/ppermute | solution.py:15
  265.7 24.3 %fusion.25 = f32[1,2,16,4,128,128]{5,4,3,2,1,0:T(8,128)S(1)} fusion(f32[1,2,16,4,128,128]{5,4,3,2,1,0:T(8,128)} %copy-done, f32[1,2,16,1,128,128]{5,4,3,2,1,0:T(8,128)} %collective-permute-done, f32[1,2,16,1,128,128]{5,4,3,2,1,0:T(8,128)} %collective-permute-done.1, f32[4,128,128]{2,1,0:T(8,128)} %get-tuple-element.259), kind=kLoop, calls=%fused_computation.8.clone.1 | loop fusion | flops 18874368 | bytes 21233664 | tf_op jit(solution)/shard_map/while/body/eval_jaxpr/sub | solution.py:29
  290.0 7.1 %add_divide_fusion.2 = (f32[1,1,16,4,128,128]{5,4,3,2,1,0:T(8,128)}, f32[1,1,16,4,128,128]{5,4,3,2,1,0:T(8,128)}) fusion(f32[4,128,128]{2,1,0:T(8,128)} %get-tuple-element.258, f32[]{:T(128)} %bitcast.45, f32[4,128,128]{2,1,0:T(8,128)} %get-tuple-element.259, f32[1,2,16,4,128,128]{5,4,3,2,1,0:T(8,128)S(1)} %bitcast.49, ...), kind=kLoop, calls=%fused_computation.22.clone.1 | loop fusion | flops 14680064 | bytes 29884420 | tf_op jit(solution)/shard_map/while/body/eval_jaxpr/div | solution.py:33
  314.2 23.2 %collective-permute-start = (f32[1,2,16,1,128,128]{5,4,3,2,1,0:T(8,128)}, f32[1,2,16,1,128,128]{5,4,3,2,1,0:T(8,128)}, u32[]{:S(2)}, u32[]{:S(2)}) collective-permute-start(f32[1,2,16,1,128,128]{5,4,3,2,1,0:T(8,128)} %get-tuple-element.260), channel_id=1, source_target_pairs={{0,1},{1,2},{2,3},{3,4},{4,5},{5,6},{6,7},{8,9},{9,10},{10,11},{11... | collective-permute-start | bytes 6291464 | tf_op jit(solution)/shard_map/while/body/eval_jaxpr/ppermute | solution.py:15
  343.6 24.3 %fusion.25 = f32[1,2,16,4,128,128]{5,4,3,2,1,0:T(8,128)S(1)} fusion(f32[1,2,16,4,128,128]{5,4,3,2,1,0:T(8,128)} %copy-done, f32[1,2,16,1,128,128]{5,4,3,2,1,0:T(8,128)} %collective-permute-done, f32[1,2,16,1,128,128]{5,4,3,2,1,0:T(8,128)} %collective-permute-done.1, f32[4,128,128]{2,1,0:T(8,128)} %get-tuple-element.259), kind=kLoop, calls=%fused_computation.8.clone.1 | loop fusion | flops 18874368 | bytes 21233664 | tf_op jit(solution)/shard_map/while/body/eval_jaxpr/sub | solution.py:29
  367.9 7.1 %add_divide_fusion.2 = (f32[1,1,16,4,128,128]{5,4,3,2,1,0:T(8,128)}, f32[1,1,16,4,128,128]{5,4,3,2,1,0:T(8,128)}) fusion(f32[4,128,128]{2,1,0:T(8,128)} %get-tuple-element.258, f32[]{:T(128)} %bitcast.45, f32[4,128,128]{2,1,0:T(8,128)} %get-tuple-element.259, f32[1,2,16,4,128,128]{5,4,3,2,1,0:T(8,128)S(1)} %bitcast.49, ...), kind=kLoop, calls=%fused_computation.22.clone.1 | loop fusion | flops 14680064 | bytes 29884420 | tf_op jit(solution)/shard_map/while/body/eval_jaxpr/div | solution.py:33
  392.2 23.2 %collective-permute-start = (f32[1,2,16,1,128,128]{5,4,3,2,1,0:T(8,128)}, f32[1,2,16,1,128,128]{5,4,3,2,1,0:T(8,128)}, u32[]{:S(2)}, u32[]{:S(2)}) collective-permute-start(f32[1,2,16,1,128,128]{5,4,3,2,1,0:T(8,128)} %get-tuple-element.260), channel_id=1, source_target_pairs={{0,1},{1,2},{2,3},{3,4},{4,5},{5,6},{6,7},{8,9},{9,10},{10,11},{11... | collective-permute-start | bytes 6291464 | tf_op jit(solution)/shard_map/while/body/eval_jaxpr/ppermute | solution.py:15
  421.6 24.3 %fusion.25 = f32[1,2,16,4,128,128]{5,4,3,2,1,0:T(8,128)S(1)} fusion(f32[1,2,16,4,128,128]{5,4,3,2,1,0:T(8,128)} %copy-done, f32[1,2,16,1,128,128]{5,4,3,2,1,0:T(8,128)} %collective-permute-done, f32[1,2,16,1,128,128]{5,4,3,2,1,0:T(8,128)} %collective-permute-done.1, f32[4,128,128]{2,1,0:T(8,128)} %get-tuple-element.259), kind=kLoop, calls=%fused_computation.8.clone.1 | loop fusion | flops 18874368 | bytes 21233664 | tf_op jit(solution)/shard_map/while/body/eval_jaxpr/sub | solution.py:29
  445.9 7.1 %add_divide_fusion.2 = (f32[1,1,16,4,128,128]{5,4,3,2,1,0:T(8,128)}, f32[1,1,16,4,128,128]{5,4,3,2,1,0:T(8,128)}) fusion(f32[4,128,128]{2,1,0:T(8,128)} %get-tuple-element.258, f32[]{:T(128)} %bitcast.45, f32[4,128,128]{2,1,0:T(8,128)} %get-tuple-element.259, f32[1,2,16,4,128,128]{5,4,3,2,1,0:T(8,128)S(1)} %bitcast.49, ...), kind=kLoop, calls=%fused_computation.22.clone.1 | loop fusion | flops 14680064 | bytes 29884420 | tf_op jit(solution)/shard_map/while/body/eval_jaxpr/div | solution.py:33
  461.0 7.5 %reshape.188 = f32[2,16,65536]{2,1,0:T(8,128)} reshape(f32[1,2,16,4,128,128]{5,4,3,2,1,0:T(8,128)} %get-tuple-element.162) | data formatting | bytes 16777216 | tf_op jit(solution)/shard_map/reshape.4
  472.4 27.3 %fusion.11 = f32[1,16,16]{2,1,0:T(8,128)S(1)} fusion(f32[2,16,4,128,128]{4,3,2,1,0:T(8,128)} %bitcast.52), kind=kOutput, calls=%fused_computation.30 | convolution fusion | flops 402653184 | bytes 8389632 | tf_op jit(solution)/shard_map/naic,najc->nij/dot_general | solution.py:62
  501.0 8.4 %convolution_bitcast_fusion.1 = f32[1,2,16,16]{3,2,1,0:T(8,128)S(1)} fusion(f32[2,16,65536]{2,1,0:T(8,128)S(1)} %copy-done.2, f32[16,65536,1]{1,0,2:T(8,128)} %reshape.196), kind=kOutput, calls=%fused_computation.29 | convolution fusion | flops 402653184 | bytes 12584960 | tf_op jit(solution)/shard_map/naic,pc->naip/dot_general | solution.py:59
  509.4 45.7 %all-reduce.1 = (f32[1,2,16,16]{3,2,1,0:T(8,128)S(1)}, f32[1,16,16]{2,1,0:T(8,128)S(1)}) all-reduce(f32[1,2,16,16]{3,2,1,0:T(8,128)S(1)} %convolution_bitcast_fusion.1, f32[1,16,16]{2,1,0:T(8,128)S(1)} %fusion.11), channel_id=1, replica_groups=mesh['node'=4,'row'=8] {'row'}, use_global_device_ids=true, to_apply=%region_4.5 | all-reduce | flops 768 | bytes 6144 | tf_op jit(solution)/shard_map/psum | solution.py:65
  555.2 8.4 %convolution_bitcast_fusion = f32[16,65536]{1,0:T(8,128)} fusion(f32[2,16,65536]{2,1,0:T(8,128)} %reshape.188, f32[1,2,16,16]{3,2,1,0:T(8,128)S(1)} %get-tuple-element.201, f32[]{:T(128)} %select_reduce_fusion), kind=kOutput, calls=%fused_computation.25 | convolution fusion | flops 402653696 | bytes 12584964 | tf_op jit(solution)/shard_map/naip,naic->pc/dot_general | solution.py:72
  564.8 100.7 %all-reduce.4.cloned.1.call-done = f32[16,65536]{1,0:T(8,128)} async-done(((f32[16,65536]{1,0:T(8,128)}), f32[16,65536]{1,0:T(8,128)}) %all-reduce.4.cloned.1.call-update) | async-done | bytes 4194320 | tf_op jit(solution)/shard_map/psum | solution.py:73
  (154 shorter events, 153.5 us)
Async XLA Ops:
  7.2 658.4 %all-reduce.4.cloned.1.call-start = ((), (), s32[]{:S(2)}) async-start(), calls=%async_computation | async-start | bytes 8388608 | tf_op jit(solution)/shard_map/psum | solution.py:73
  19.3 6.6 collective-permute-start
  23.0 7.0 %collective-permute-start.1 = (f32[1,2,16,1,128,128]{5,4,3,2,1,0:T(8,128)S(1)}, f32[1,2,16,1,128,128]{5,4,3,2,1,0:T(8,128)}, u32[]{:S(2)}, u32[]{:S(2)}) collective-permute-start(f32[1,2,16,1,128,128]{5,4,3,2,1,0:T(8,128)S(1)} %get-tuple-element.261), channel_id=1, source_target_pairs={{1,0},{2,1},{3,2},{4,3},{5,4},{6,5},{7,6},{9,8},{10,9},{11,10},{12... | collective-permute-start | bytes 6291464 | tf_op jit(solution)/shard_map/while/body/eval_jaxpr/ppermute | solution.py:18
  25.0 29.3 %slice-start = ((s8[8388608]{0:T(1024)(128)(4,1)}), s8[4194304]{0:T(1024)(128)(4,1)S(1)}, s32[]{:S(2)}) async-start(s8[8388608]{0:T(1024)(128)(4,1)} %bitcast.48), calls=%async_computation.1 | async-start | bytes 8388608 | tf_op jit(solution)/shard_map/while
  30.0 31.5 %slice-start.2 = ((s8[8388608]{0:T(1024)(128)(4,1)}), s8[4194304]{0:T(1024)(128)(4,1)S(1)}, s32[]{:S(2)}) async-start(s8[8388608]{0:T(1024)(128)(4,1)} %bitcast.50), calls=%async_computation.3 | async-start | bytes 8388608 | tf_op jit(solution)/shard_map/while
  76.9 28.7 %copy-start.3 = (f32[4,128,128]{2,1,0:T(8,128)S(1)}, f32[4,128,128]{2,1,0:T(8,128)}, u32[]{:S(2)}) copy-start(f32[4,128,128]{2,1,0:T(8,128)} %get-tuple-element.285) | copy-start | bytes 786436 | tf_op jit(solution)/shard_map/while
  78.6 27.9 %collective-permute-start = (f32[1,2,16,1,128,128]{5,4,3,2,1,0:T(8,128)}, f32[1,2,16,1,128,128]{5,4,3,2,1,0:T(8,128)}, u32[]{:S(2)}, u32[]{:S(2)}) collective-permute-start(f32[1,2,16,1,128,128]{5,4,3,2,1,0:T(8,128)} %get-tuple-element.260), channel_id=1, source_target_pairs={{0,1},{1,2},{2,3},{3,4},{4,5},{5,6},{6,7},{8,9},{9,10},{10,11},{11... | collective-permute-start | bytes 6291464 | tf_op jit(solution)/shard_map/while/body/eval_jaxpr/ppermute | solution.py:15
  103.6 6.2 collective-permute-start.1
  105.6 28.5 %slice-start = ((s8[8388608]{0:T(1024)(128)(4,1)}), s8[4194304]{0:T(1024)(128)(4,1)S(1)}, s32[]{:S(2)}) async-start(s8[8388608]{0:T(1024)(128)(4,1)} %bitcast.48), calls=%async_computation.1 | async-start | bytes 8388608 | tf_op jit(solution)/shard_map/while
  109.8 31.5 %slice-start.2 = ((s8[8388608]{0:T(1024)(128)(4,1)}), s8[4194304]{0:T(1024)(128)(4,1)S(1)}, s32[]{:S(2)}) async-start(s8[8388608]{0:T(1024)(128)(4,1)} %bitcast.50), calls=%async_computation.3 | async-start | bytes 8388608 | tf_op jit(solution)/shard_map/while
  158.3 26.0 %collective-permute-start = (f32[1,2,16,1,128,128]{5,4,3,2,1,0:T(8,128)}, f32[1,2,16,1,128,128]{5,4,3,2,1,0:T(8,128)}, u32[]{:S(2)}, u32[]{:S(2)}) collective-permute-start(f32[1,2,16,1,128,128]{5,4,3,2,1,0:T(8,128)} %get-tuple-element.260), channel_id=1, source_target_pairs={{0,1},{1,2},{2,3},{3,4},{4,5},{5,6},{6,7},{8,9},{9,10},{10,11},{11... | collective-permute-start | bytes 6291464 | tf_op jit(solution)/shard_map/while/body/eval_jaxpr/ppermute | solution.py:15
  181.5 6.2 collective-permute-start.1
  187.7 31.5 %slice-start.2 = ((s8[8388608]{0:T(1024)(128)(4,1)}), s8[4194304]{0:T(1024)(128)(4,1)S(1)}, s32[]{:S(2)}) async-start(s8[8388608]{0:T(1024)(128)(4,1)} %bitcast.50), calls=%async_computation.3 | async-start | bytes 8388608 | tf_op jit(solution)/shard_map/while
  236.3 26.0 %collective-permute-start = (f32[1,2,16,1,128,128]{5,4,3,2,1,0:T(8,128)}, f32[1,2,16,1,128,128]{5,4,3,2,1,0:T(8,128)}, u32[]{:S(2)}, u32[]{:S(2)}) collective-permute-start(f32[1,2,16,1,128,128]{5,4,3,2,1,0:T(8,128)} %get-tuple-element.260), channel_id=1, source_target_pairs={{0,1},{1,2},{2,3},{3,4},{4,5},{5,6},{6,7},{8,9},{9,10},{10,11},{11... | collective-permute-start | bytes 6291464 | tf_op jit(solution)/shard_map/while/body/eval_jaxpr/ppermute | solution.py:15
  259.5 6.2 collective-permute-start.1
  265.7 31.5 %slice-start.2 = ((s8[8388608]{0:T(1024)(128)(4,1)}), s8[4194304]{0:T(1024)(128)(4,1)S(1)}, s32[]{:S(2)}) async-start(s8[8388608]{0:T(1024)(128)(4,1)} %bitcast.50), calls=%async_computation.3 | async-start | bytes 8388608 | tf_op jit(solution)/shard_map/while
  314.2 26.0 %collective-permute-start = (f32[1,2,16,1,128,128]{5,4,3,2,1,0:T(8,128)}, f32[1,2,16,1,128,128]{5,4,3,2,1,0:T(8,128)}, u32[]{:S(2)}, u32[]{:S(2)}) collective-permute-start(f32[1,2,16,1,128,128]{5,4,3,2,1,0:T(8,128)} %get-tuple-element.260), channel_id=1, source_target_pairs={{0,1},{1,2},{2,3},{3,4},{4,5},{5,6},{6,7},{8,9},{9,10},{10,11},{11... | collective-permute-start | bytes 6291464 | tf_op jit(solution)/shard_map/while/body/eval_jaxpr/ppermute | solution.py:15
  337.4 6.2 collective-permute-start.1
  343.6 31.5 %slice-start.2 = ((s8[8388608]{0:T(1024)(128)(4,1)}), s8[4194304]{0:T(1024)(128)(4,1)S(1)}, s32[]{:S(2)}) async-start(s8[8388608]{0:T(1024)(128)(4,1)} %bitcast.50), calls=%async_computation.3 | async-start | bytes 8388608 | tf_op jit(solution)/shard_map/while
  392.2 26.0 %collective-permute-start = (f32[1,2,16,1,128,128]{5,4,3,2,1,0:T(8,128)}, f32[1,2,16,1,128,128]{5,4,3,2,1,0:T(8,128)}, u32[]{:S(2)}, u32[]{:S(2)}) collective-permute-start(f32[1,2,16,1,128,128]{5,4,3,2,1,0:T(8,128)} %get-tuple-element.260), channel_id=1, source_target_pairs={{0,1},{1,2},{2,3},{3,4},{4,5},{5,6},{6,7},{8,9},{9,10},{10,11},{11... | collective-permute-start | bytes 6291464 | tf_op jit(solution)/shard_map/while/body/eval_jaxpr/ppermute | solution.py:15
  415.4 6.2 collective-permute-start.1
  421.6 31.5 %slice-start.2 = ((s8[8388608]{0:T(1024)(128)(4,1)}), s8[4194304]{0:T(1024)(128)(4,1)S(1)}, s32[]{:S(2)}) async-start(s8[8388608]{0:T(1024)(128)(4,1)} %bitcast.50), calls=%async_computation.3 | async-start | bytes 8388608 | tf_op jit(solution)/shard_map/while
  468.5 31.3 %copy-start.4 = (f32[4]{0:T(128)S(1)}, f32[4]{0:T(128)}, u32[]{:S(2)}) copy-start(f32[4]{0:T(128)} %param.13) | copy-start | bytes 52
  472.4 28.5 %copy-start.2 = (f32[2,16,65536]{2,1,0:T(8,128)S(1)}, f32[2,16,65536]{2,1,0:T(8,128)}, u32[]{:S(2)}) copy-start(f32[2,16,65536]{2,1,0:T(8,128)} %reshape.188) | copy-start | bytes 25165828
  (33 other events, 456.3 us)
Sparse Core Ops, SparseCore 0:
  563.7 101.8 all-reduce.3
where the time goes:
time: 678 us
  other arithmetic  252 us (37%)
  starting transfers between devices  129 us (19%)
  waiting for transfers between devices  122 us (18%)
  local copies, waits for them, and re-layouts  64.7 us (10%)
  blocking collectives  45.7 us (7%)
  matrix products  44.1 us (7%)
  between operations  15.2 us (2%)
    sub x6, other arithmetic, relax_step(): applied = diag_full * fields - beside  146 us
    ppermute x6, starting transfers between devices, with_halo(): lax.ppermute(lax.slice_in_dim(block, block.shape[dim] - width, None, axis...  122 us
    psum x1, waiting for transfers between devices, local(): summed = lax.psum(share, 'node')  101 us
    psum x1, blocking collectives, local(): projected, gram_part = lax.psum((projected, gram_part), 'row')  45.7 us
    div x6, other arithmetic, relax_step(): step_real = (diag_full * resid_real + shift_col * resid_imag) / denominator  42.9 us
    while x84, local copies, waits for them, and re-layouts  38.8 us
    add x6, other arithmetic, relax_step(): return fields + active * jnp.stack([step_real, step_imag], 1)  28 us
    dot_general x1, matrix products, local(): jnp.einsum('naic,najc->nij', flat_fields, flat_fields, precision=lax.Prec...  27.3 us
  transfers between devices with their start and end apart: 13, of which 7 were waited for; matrix products, arithmetic and copies ran while one was open for 1% of the time, Pallas kernels for 0%

commit v1 on v0

--- a/solution.py
+++ b/solution.py
@@ -70,7 +70,9 @@
     )
     weighted = projected * my_weights.reshape(NODE_DEV, 1, 1, 1)
     share = jnp.einsum("naip,naic->pc", weighted, flat_fields, precision=lax.Precision.HIGHEST)
-    summed = lax.psum(share, "node")
+    summed = share
+    for hop in (1, 2):
+        summed = summed + lax.ppermute(summed, "node", [(dev, dev ^ hop) for dev in range(4)])
     probe_response = (summed / quad_count).reshape(observations.shape)
     return (probe_response, group_gram[None])
 

time: 678 us -> 747 us (1.10)
  waiting for transfers between devices: 122 us -> 200 us
  between operations: 15.2 us -> 1.95 us
    ppermute x0 -> x2, waiting for transfers between devices: none -> 173 us  [local(): lax.ppermute(summed, 'node', [(dev, dev ^ hop) for dev in range(4)])]
    psum x1 -> x0, waiting for transfers between devices: 101 us -> none  [local(): summed = lax.psum(share, 'node')]
  transfers between devices with their start and end apart: 13 -> 14, of which waited for: 7 -> 14; matrix products, arithmetic and copies ran while one was open for 1% -> 0% of each run, Pallas kernels for 0% -> 0%
where the time goes in v1:
time: 747 us; the launch traced here: 744 us
  other arithmetic  255 us (34%)
  waiting for transfers between devices  200 us (27%)
  starting transfers between devices  132 us (18%)
  local copies, waits for them, and re-layouts  61.8 us (8%)
  blocking collectives  45.8 us (6%)
  matrix products  43.1 us (6%)
    ppermute x2, waiting for transfers between devices, local(): lax.ppermute(summed, 'node', [(dev, dev ^ hop) for dev in range(4)])  173 us
    sub x6, other arithmetic, relax_step(): applied = diag_full * fields - beside  144 us
    ppermute x6, starting transfers between devices, with_halo(): lax.ppermute(lax.slice_in_dim(block, block.shape[dim] - width, None, axis...  122 us
    div x6, other arithmetic, relax_step(): step_real = (diag_full * resid_real + shift_col * resid_imag) / denominator  49.2 us
    psum x1, blocking collectives, local(): projected, gram_part = lax.psum((projected, gram_part), 'row')  45.8 us
    add x6, other arithmetic, relax_step(): return fields + active * jnp.stack([step_real, step_imag], 1)  32.2 us
    while x84, local copies, waits for them, and re-layouts  31.7 us
    dot_general x1, matrix products, local(): jnp.einsum('naic,najc->nij', flat_fields, flat_fields, precision=lax.Prec...  27.4 us
  transfers between devices with their start and end apart: 14, of which 14 were waited for; matrix products, arithmetic and copies ran while one was open for 0% of the time, Pallas kernels for 0%

profile of v1, /device:TPU:0, one launch (start us, length us, event | category | flops | bytes accessed | tf_op | source)
XLA Modules:
  0.0 744.0 jit_solution(18044328120440762440)
XLA Ops:
  7.1 454.6 %while.16 = (s32[]{:T(128)}, f32[1,2,16,4,128,128]{5,4,3,2,1,0:T(8,128)}, s32[1]{0:T(128)}, f32[4,128,128]{2,1,0:T(8,128)}, f32[16,4,128,128]{3,2,1,0:T(8,128)},...) while((s32[]{:T(128)}, ...), condition=%wide.region_3.4_spmd.clone, body=%wide.region_2.3_spmd.clone.sunk | while | flops 44236800 | bytes 237502864 | solution.py:55
  23.4 23.9 %fusion.25 = f32[1,2,16,4,128,128]{5,4,3,2,1,0:T(8,128)S(1)} fusion(f32[1,2,16,4,128,128]{5,4,3,2,1,0:T(8,128)} %copy-done, f32[1,2,16,1,128,128]{5,4,3,2,1,0:T(8,128)} %collective-permute-done, f32[1,2,16,1,128,128]{5,4,3,2,1,0:T(8,128)} %collective-permute-done.1, f32[4,128,128]{2,1,0:T(8,128)S(1)} %get-tuple-element.259), kind=kLoop, calls=%fused_computation.8.clone.1 | loop fusion | flops 18874368 | bytes 21233664 | tf_op jit(solution)/shard_map/while/body/eval_jaxpr/sub | solution.py:29
  47.4 8.2 %add_divide_fusion.2 = (f32[1,1,16,4,128,128]{5,4,3,2,1,0:T(8,128)}, f32[1,1,16,4,128,128]{5,4,3,2,1,0:T(8,128)}) fusion(f32[4,128,128]{2,1,0:T(8,128)S(1)} %get-tuple-element.258, f32[]{:T(128)} %bitcast.45, f32[4,128,128]{2,1,0:T(8,128)S(1)} %get-tuple-element.259, f32[1,2,16,4,128,128]{5,4,3,2,1,0:T(8,128)S(1)} %bitcast.49, ...), kind=kLoop, calls=%fused_computation.22.clone.1 | loop fusion | flops 14680064 | bytes 29884420 | tf_op jit(solution)/shard_map/while/body/eval_jaxpr/div | solution.py:33
  72.9 25.0 %collective-permute-start = (f32[1,2,16,1,128,128]{5,4,3,2,1,0:T(8,128)}, f32[1,2,16,1,128,128]{5,4,3,2,1,0:T(8,128)}, u32[]{:S(2)}, u32[]{:S(2)}) collective-permute-start(f32[1,2,16,1,128,128]{5,4,3,2,1,0:T(8,128)} %get-tuple-element.260), channel_id=1, source_target_pairs={{0,1},{1,2},{2,3},{3,4},{4,5},{5,6},{6,7},{8,9},{9,10},{10,11},{11... | collective-permute-start | bytes 6291464 | tf_op jit(solution)/shard_map/while/body/eval_jaxpr/ppermute | solution.py:15
  104.3 23.9 %fusion.25 = f32[1,2,16,4,128,128]{5,4,3,2,1,0:T(8,128)S(1)} fusion(f32[1,2,16,4,128,128]{5,4,3,2,1,0:T(8,128)} %copy-done, f32[1,2,16,1,128,128]{5,4,3,2,1,0:T(8,128)} %collective-permute-done, f32[1,2,16,1,128,128]{5,4,3,2,1,0:T(8,128)} %collective-permute-done.1, f32[4,128,128]{2,1,0:T(8,128)S(1)} %get-tuple-element.259), kind=kLoop, calls=%fused_computation.8.clone.1 | loop fusion | flops 18874368 | bytes 21233664 | tf_op jit(solution)/shard_map/while/body/eval_jaxpr/sub | solution.py:29
  128.3 8.2 %add_divide_fusion.2 = (f32[1,1,16,4,128,128]{5,4,3,2,1,0:T(8,128)}, f32[1,1,16,4,128,128]{5,4,3,2,1,0:T(8,128)}) fusion(f32[4,128,128]{2,1,0:T(8,128)S(1)} %get-tuple-element.258, f32[]{:T(128)} %bitcast.45, f32[4,128,128]{2,1,0:T(8,128)S(1)} %get-tuple-element.259, f32[1,2,16,4,128,128]{5,4,3,2,1,0:T(8,128)S(1)} %bitcast.49, ...), kind=kLoop, calls=%fused_computation.22.clone.1 | loop fusion | flops 14680064 | bytes 29884420 | tf_op jit(solution)/shard_map/while/body/eval_jaxpr/div | solution.py:33
  153.9 23.2 %collective-permute-start = (f32[1,2,16,1,128,128]{5,4,3,2,1,0:T(8,128)}, f32[1,2,16,1,128,128]{5,4,3,2,1,0:T(8,128)}, u32[]{:S(2)}, u32[]{:S(2)}) collective-permute-start(f32[1,2,16,1,128,128]{5,4,3,2,1,0:T(8,128)} %get-tuple-element.260), channel_id=1, source_target_pairs={{0,1},{1,2},{2,3},{3,4},{4,5},{5,6},{6,7},{8,9},{9,10},{10,11},{11... | collective-permute-start | bytes 6291464 | tf_op jit(solution)/shard_map/while/body/eval_jaxpr/ppermute | solution.py:15
  183.5 23.9 %fusion.25 = f32[1,2,16,4,128,128]{5,4,3,2,1,0:T(8,128)S(1)} fusion(f32[1,2,16,4,128,128]{5,4,3,2,1,0:T(8,128)} %copy-done, f32[1,2,16,1,128,128]{5,4,3,2,1,0:T(8,128)} %collective-permute-done, f32[1,2,16,1,128,128]{5,4,3,2,1,0:T(8,128)} %collective-permute-done.1, f32[4,128,128]{2,1,0:T(8,128)S(1)} %get-tuple-element.259), kind=kLoop, calls=%fused_computation.8.clone.1 | loop fusion | flops 18874368 | bytes 21233664 | tf_op jit(solution)/shard_map/while/body/eval_jaxpr/sub | solution.py:29
  207.5 8.2 %add_divide_fusion.2 = (f32[1,1,16,4,128,128]{5,4,3,2,1,0:T(8,128)}, f32[1,1,16,4,128,128]{5,4,3,2,1,0:T(8,128)}) fusion(f32[4,128,128]{2,1,0:T(8,128)S(1)} %get-tuple-element.258, f32[]{:T(128)} %bitcast.45, f32[4,128,128]{2,1,0:T(8,128)S(1)} %get-tuple-element.259, f32[1,2,16,4,128,128]{5,4,3,2,1,0:T(8,128)S(1)} %bitcast.49, ...), kind=kLoop, calls=%fused_computation.22.clone.1 | loop fusion | flops 14680064 | bytes 29884420 | tf_op jit(solution)/shard_map/while/body/eval_jaxpr/div | solution.py:33
  233.0 23.2 %collective-permute-start = (f32[1,2,16,1,128,128]{5,4,3,2,1,0:T(8,128)}, f32[1,2,16,1,128,128]{5,4,3,2,1,0:T(8,128)}, u32[]{:S(2)}, u32[]{:S(2)}) collective-permute-start(f32[1,2,16,1,128,128]{5,4,3,2,1,0:T(8,128)} %get-tuple-element.260), channel_id=1, source_target_pairs={{0,1},{1,2},{2,3},{3,4},{4,5},{5,6},{6,7},{8,9},{9,10},{10,11},{11... | collective-permute-start | bytes 6291464 | tf_op jit(solution)/shard_map/while/body/eval_jaxpr/ppermute | solution.py:15
  262.6 23.9 %fusion.25 = f32[1,2,16,4,128,128]{5,4,3,2,1,0:T(8,128)S(1)} fusion(f32[1,2,16,4,128,128]{5,4,3,2,1,0:T(8,128)} %copy-done, f32[1,2,16,1,128,128]{5,4,3,2,1,0:T(8,128)} %collective-permute-done, f32[1,2,16,1,128,128]{5,4,3,2,1,0:T(8,128)} %collective-permute-done.1, f32[4,128,128]{2,1,0:T(8,128)S(1)} %get-tuple-element.259), kind=kLoop, calls=%fused_computation.8.clone.1 | loop fusion | flops 18874368 | bytes 21233664 | tf_op jit(solution)/shard_map/while/body/eval_jaxpr/sub | solution.py:29
  286.6 8.2 %add_divide_fusion.2 = (f32[1,1,16,4,128,128]{5,4,3,2,1,0:T(8,128)}, f32[1,1,16,4,128,128]{5,4,3,2,1,0:T(8,128)}) fusion(f32[4,128,128]{2,1,0:T(8,128)S(1)} %get-tuple-element.258, f32[]{:T(128)} %bitcast.45, f32[4,128,128]{2,1,0:T(8,128)S(1)} %get-tuple-element.259, f32[1,2,16,4,128,128]{5,4,3,2,1,0:T(8,128)S(1)} %bitcast.49, ...), kind=kLoop, calls=%fused_computation.22.clone.1 | loop fusion | flops 14680064 | bytes 29884420 | tf_op jit(solution)/shard_map/while/body/eval_jaxpr/div | solution.py:33
  312.1 23.2 %collective-permute-start = (f32[1,2,16,1,128,128]{5,4,3,2,1,0:T(8,128)}, f32[1,2,16,1,128,128]{5,4,3,2,1,0:T(8,128)}, u32[]{:S(2)}, u32[]{:S(2)}) collective-permute-start(f32[1,2,16,1,128,128]{5,4,3,2,1,0:T(8,128)} %get-tuple-element.260), channel_id=1, source_target_pairs={{0,1},{1,2},{2,3},{3,4},{4,5},{5,6},{6,7},{8,9},{9,10},{10,11},{11... | collective-permute-start | bytes 6291464 | tf_op jit(solution)/shard_map/while/body/eval_jaxpr/ppermute | solution.py:15
  341.7 23.9 %fusion.25 = f32[1,2,16,4,128,128]{5,4,3,2,1,0:T(8,128)S(1)} fusion(f32[1,2,16,4,128,128]{5,4,3,2,1,0:T(8,128)} %copy-done, f32[1,2,16,1,128,128]{5,4,3,2,1,0:T(8,128)} %collective-permute-done, f32[1,2,16,1,128,128]{5,4,3,2,1,0:T(8,128)} %collective-permute-done.1, f32[4,128,128]{2,1,0:T(8,128)S(1)} %get-tuple-element.259), kind=kLoop, calls=%fused_computation.8.clone.1 | loop fusion | flops 18874368 | bytes 21233664 | tf_op jit(solution)/shard_map/while/body/eval_jaxpr/sub | solution.py:29
  365.7 8.2 %add_divide_fusion.2 = (f32[1,1,16,4,128,128]{5,4,3,2,1,0:T(8,128)}, f32[1,1,16,4,128,128]{5,4,3,2,1,0:T(8,128)}) fusion(f32[4,128,128]{2,1,0:T(8,128)S(1)} %get-tuple-element.258, f32[]{:T(128)} %bitcast.45, f32[4,128,128]{2,1,0:T(8,128)S(1)} %get-tuple-element.259, f32[1,2,16,4,128,128]{5,4,3,2,1,0:T(8,128)S(1)} %bitcast.49, ...), kind=kLoop, calls=%fused_computation.22.clone.1 | loop fusion | flops 14680064 | bytes 29884420 | tf_op jit(solution)/shard_map/while/body/eval_jaxpr/div | solution.py:33
  391.3 23.2 %collective-permute-start = (f32[1,2,16,1,128,128]{5,4,3,2,1,0:T(8,128)}, f32[1,2,16,1,128,128]{5,4,3,2,1,0:T(8,128)}, u32[]{:S(2)}, u32[]{:S(2)}) collective-permute-start(f32[1,2,16,1,128,128]{5,4,3,2,1,0:T(8,128)} %get-tuple-element.260), channel_id=1, source_target_pairs={{0,1},{1,2},{2,3},{3,4},{4,5},{5,6},{6,7},{8,9},{9,10},{10,11},{11... | collective-permute-start | bytes 6291464 | tf_op jit(solution)/shard_map/while/body/eval_jaxpr/ppermute | solution.py:15
  420.9 23.9 %fusion.25 = f32[1,2,16,4,128,128]{5,4,3,2,1,0:T(8,128)S(1)} fusion(f32[1,2,16,4,128,128]{5,4,3,2,1,0:T(8,128)} %copy-done, f32[1,2,16,1,128,128]{5,4,3,2,1,0:T(8,128)} %collective-permute-done, f32[1,2,16,1,128,128]{5,4,3,2,1,0:T(8,128)} %collective-permute-done.1, f32[4,128,128]{2,1,0:T(8,128)S(1)} %get-tuple-element.259), kind=kLoop, calls=%fused_computation.8.clone.1 | loop fusion | flops 18874368 | bytes 21233664 | tf_op jit(solution)/shard_map/while/body/eval_jaxpr/sub | solution.py:29
  444.9 8.2 %add_divide_fusion.2 = (f32[1,1,16,4,128,128]{5,4,3,2,1,0:T(8,128)}, f32[1,1,16,4,128,128]{5,4,3,2,1,0:T(8,128)}) fusion(f32[4,128,128]{2,1,0:T(8,128)S(1)} %get-tuple-element.258, f32[]{:T(128)} %bitcast.45, f32[4,128,128]{2,1,0:T(8,128)S(1)} %get-tuple-element.259, f32[1,2,16,4,128,128]{5,4,3,2,1,0:T(8,128)S(1)} %bitcast.49, ...), kind=kLoop, calls=%fused_computation.22.clone.1 | loop fusion | flops 14680064 | bytes 29884420 | tf_op jit(solution)/shard_map/while/body/eval_jaxpr/div | solution.py:33
  461.7 7.5 %reshape.188 = f32[2,16,65536]{2,1,0:T(8,128)} reshape(f32[1,2,16,4,128,128]{5,4,3,2,1,0:T(8,128)} %get-tuple-element.162) | data formatting | bytes 16777216 | tf_op jit(solution)/shard_map/reshape.4
  473.2 27.4 %fusion.11 = f32[1,16,16]{2,1,0:T(8,128)S(1)} fusion(f32[2,16,4,128,128]{4,3,2,1,0:T(8,128)} %bitcast.52), kind=kOutput, calls=%fused_computation.30 | convolution fusion | flops 402653184 | bytes 8389632 | tf_op jit(solution)/shard_map/naic,najc->nij/dot_general | solution.py:62
  501.9 8.4 %convolution_bitcast_fusion.1 = f32[1,2,16,16]{3,2,1,0:T(8,128)S(1)} fusion(f32[2,16,65536]{2,1,0:T(8,128)S(1)} %copy-done.2, f32[16,65536,1]{1,0,2:T(8,128)} %reshape.196), kind=kOutput, calls=%fused_computation.29 | convolution fusion | flops 402653184 | bytes 12584960 | tf_op jit(solution)/shard_map/naic,pc->naip/dot_general | solution.py:59
  510.3 45.8 %all-reduce.1 = (f32[1,2,16,16]{3,2,1,0:T(8,128)S(1)}, f32[1,16,16]{2,1,0:T(8,128)S(1)}) all-reduce(f32[1,2,16,16]{3,2,1,0:T(8,128)S(1)} %convolution_bitcast_fusion.1, f32[1,16,16]{2,1,0:T(8,128)S(1)} %fusion.11), channel_id=1, replica_groups=mesh['node'=4,'row'=8] {'row'}, use_global_device_ids=true, to_apply=%region_4.5 | all-reduce | flops 768 | bytes 6144 | tf_op jit(solution)/shard_map/psum | solution.py:65
  564.9 87.4 %collective-permute-done.2 = f32[16,65536]{1,0:T(8,128)S(1)} collective-permute-done((f32[16,65536]{1,0:T(8,128)S(1)}, f32[16,65536]{1,0:T(8,128)S(1)}, u32[]{:S(2)}, u32[]{:S(2)}) %collective-permute-start.2) | collective-permute-done | bytes 4194336 | tf_op jit(solution)/shard_map/ppermute | solution.py:75
  655.5 85.3 %collective-permute-done.3 = f32[16,65536]{1,0:T(8,128)S(1)} collective-permute-done((f32[16,65536]{1,0:T(8,128)S(1)}, f32[16,65536]{1,0:T(8,128)S(1)}, u32[]{:S(2)}, u32[]{:S(2)}) %collective-permute-start.3) | collective-permute-done | bytes 4194336 | tf_op jit(solution)/shard_map/ppermute | solution.py:75
  (156 shorter events, 165.1 us)
Async XLA Ops:
  12.4 6.5 collective-permute-start
  16.1 7.3 collective-permute-start.1
  23.4 24.0 %slice-start.1 = ((s8[8388608]{0:T(1024)(128)(4,1)}), s8[4194304]{0:T(1024)(128)(4,1)S(1)}, s32[]{:S(2)}) async-start(s8[8388608]{0:T(1024)(128)(4,1)} %bitcast.48), calls=%async_computation.1 | async-start | bytes 8388608 | tf_op jit(solution)/shard_map/while
  68.5 31.4 %copy-start.3 = (f32[4,128,128]{2,1,0:T(8,128)S(1)}, f32[4,128,128]{2,1,0:T(8,128)}, u32[]{:S(2)}) copy-start(f32[4,128,128]{2,1,0:T(8,128)} %get-tuple-element.285) | copy-start | bytes 786436 | tf_op jit(solution)/shard_map/while
  72.9 27.8 %collective-permute-start = (f32[1,2,16,1,128,128]{5,4,3,2,1,0:T(8,128)}, f32[1,2,16,1,128,128]{5,4,3,2,1,0:T(8,128)}, u32[]{:S(2)}, u32[]{:S(2)}) collective-permute-start(f32[1,2,16,1,128,128]{5,4,3,2,1,0:T(8,128)} %get-tuple-element.260), channel_id=1, source_target_pairs={{0,1},{1,2},{2,3},{3,4},{4,5},{5,6},{6,7},{8,9},{9,10},{10,11},{11... | collective-permute-start | bytes 6291464 | tf_op jit(solution)/shard_map/while/body/eval_jaxpr/ppermute | solution.py:15
  97.9 6.4 collective-permute-start.1
  104.3 24.0 %slice-start.1 = ((s8[8388608]{0:T(1024)(128)(4,1)}), s8[4194304]{0:T(1024)(128)(4,1)S(1)}, s32[]{:S(2)}) async-start(s8[8388608]{0:T(1024)(128)(4,1)} %bitcast.48), calls=%async_computation.1 | async-start | bytes 8388608 | tf_op jit(solution)/shard_map/while
  149.4 29.6 %copy-start.3 = (f32[4,128,128]{2,1,0:T(8,128)S(1)}, f32[4,128,128]{2,1,0:T(8,128)}, u32[]{:S(2)}) copy-start(f32[4,128,128]{2,1,0:T(8,128)} %get-tuple-element.285) | copy-start | bytes 786436 | tf_op jit(solution)/shard_map/while
  153.9 26.0 %collective-permute-start = (f32[1,2,16,1,128,128]{5,4,3,2,1,0:T(8,128)}, f32[1,2,16,1,128,128]{5,4,3,2,1,0:T(8,128)}, u32[]{:S(2)}, u32[]{:S(2)}) collective-permute-start(f32[1,2,16,1,128,128]{5,4,3,2,1,0:T(8,128)} %get-tuple-element.260), channel_id=1, source_target_pairs={{0,1},{1,2},{2,3},{3,4},{4,5},{5,6},{6,7},{8,9},{9,10},{10,11},{11... | collective-permute-start | bytes 6291464 | tf_op jit(solution)/shard_map/while/body/eval_jaxpr/ppermute | solution.py:15
  177.1 6.4 collective-permute-start.1
  183.4 24.0 %slice-start.1 = ((s8[8388608]{0:T(1024)(128)(4,1)}), s8[4194304]{0:T(1024)(128)(4,1)S(1)}, s32[]{:S(2)}) async-start(s8[8388608]{0:T(1024)(128)(4,1)} %bitcast.48), calls=%async_computation.1 | async-start | bytes 8388608 | tf_op jit(solution)/shard_map/while
  228.5 29.6 %copy-start.3 = (f32[4,128,128]{2,1,0:T(8,128)S(1)}, f32[4,128,128]{2,1,0:T(8,128)}, u32[]{:S(2)}) copy-start(f32[4,128,128]{2,1,0:T(8,128)} %get-tuple-element.285) | copy-start | bytes 786436 | tf_op jit(solution)/shard_map/while
  233.0 26.0 %collective-permute-start = (f32[1,2,16,1,128,128]{5,4,3,2,1,0:T(8,128)}, f32[1,2,16,1,128,128]{5,4,3,2,1,0:T(8,128)}, u32[]{:S(2)}, u32[]{:S(2)}) collective-permute-start(f32[1,2,16,1,128,128]{5,4,3,2,1,0:T(8,128)} %get-tuple-element.260), channel_id=1, source_target_pairs={{0,1},{1,2},{2,3},{3,4},{4,5},{5,6},{6,7},{8,9},{9,10},{10,11},{11... | collective-permute-start | bytes 6291464 | tf_op jit(solution)/shard_map/while/body/eval_jaxpr/ppermute | solution.py:15
  256.2 6.4 collective-permute-start.1
  307.7 29.6 %copy-start.3 = (f32[4,128,128]{2,1,0:T(8,128)S(1)}, f32[4,128,128]{2,1,0:T(8,128)}, u32[]{:S(2)}) copy-start(f32[4,128,128]{2,1,0:T(8,128)} %get-tuple-element.285) | copy-start | bytes 786436 | tf_op jit(solution)/shard_map/while
  312.1 26.0 %collective-permute-start = (f32[1,2,16,1,128,128]{5,4,3,2,1,0:T(8,128)}, f32[1,2,16,1,128,128]{5,4,3,2,1,0:T(8,128)}, u32[]{:S(2)}, u32[]{:S(2)}) collective-permute-start(f32[1,2,16,1,128,128]{5,4,3,2,1,0:T(8,128)} %get-tuple-element.260), channel_id=1, source_target_pairs={{0,1},{1,2},{2,3},{3,4},{4,5},{5,6},{6,7},{8,9},{9,10},{10,11},{11... | collective-permute-start | bytes 6291464 | tf_op jit(solution)/shard_map/while/body/eval_jaxpr/ppermute | solution.py:15
  335.3 6.4 collective-permute-start.1
  386.8 29.6 %copy-start.3 = (f32[4,128,128]{2,1,0:T(8,128)S(1)}, f32[4,128,128]{2,1,0:T(8,128)}, u32[]{:S(2)}) copy-start(f32[4,128,128]{2,1,0:T(8,128)} %get-tuple-element.285) | copy-start | bytes 786436 | tf_op jit(solution)/shard_map/while
  391.3 26.0 %collective-permute-start = (f32[1,2,16,1,128,128]{5,4,3,2,1,0:T(8,128)}, f32[1,2,16,1,128,128]{5,4,3,2,1,0:T(8,128)}, u32[]{:S(2)}, u32[]{:S(2)}) collective-permute-start(f32[1,2,16,1,128,128]{5,4,3,2,1,0:T(8,128)} %get-tuple-element.260), channel_id=1, source_target_pairs={{0,1},{1,2},{2,3},{3,4},{4,5},{5,6},{6,7},{8,9},{9,10},{10,11},{11... | collective-permute-start | bytes 6291464 | tf_op jit(solution)/shard_map/while/body/eval_jaxpr/ppermute | solution.py:15
  414.5 6.4 collective-permute-start.1
  473.2 27.4 %copy-start.4 = (f32[4]{0:T(128)S(1)}, f32[4]{0:T(128)}, u32[]{:S(2)}) copy-start(f32[4]{0:T(128)} %param.13) | copy-start | bytes 52
  473.2 28.8 %copy-start.2 = (f32[2,16,65536]{2,1,0:T(8,128)S(1)}, f32[2,16,65536]{2,1,0:T(8,128)}, u32[]{:S(2)}) copy-start(f32[2,16,65536]{2,1,0:T(8,128)} %reshape.188) | copy-start | bytes 25165828
  563.3 88.9 %collective-permute-start.2 = (f32[16,65536]{1,0:T(8,128)S(1)}, f32[16,65536]{1,0:T(8,128)S(1)}, u32[]{:S(2)}, u32[]{:S(2)}) collective-permute-start(f32[16,65536]{1,0:T(8,128)S(1)} %convolution_bitcast_fusion), channel_id=1, source_target_pairs={{0,8},{8,0},{16,24},{24,16},{1,9},{9,1},{17,25},{25,17},{2,10},{10... | collective-permute-start | bytes 12582920 | tf_op jit(solution)/shard_map/ppermute | solution.py:75
  652.7 88.1 %collective-permute-start.3 = (f32[16,65536]{1,0:T(8,128)S(1)}, f32[16,65536]{1,0:T(8,128)S(1)}, u32[]{:S(2)}, u32[]{:S(2)}) collective-permute-start(f32[16,65536]{1,0:T(8,128)S(1)} %add.186), channel_id=1, source_target_pairs={{0,16},{8,24},{16,0},{24,8},{1,17},{9,25},{17,1},{25,9},{2,18},{10... | collective-permute-start | bytes 12582920 | tf_op jit(solution)/shard_map/ppermute | solution.py:75
  (34 other events, 371.0 us)
